TPU v7x, 128 devices: a whole 4x4x4 slice. The times are simulated.
128 devices in a mesh: seq: 32 (over y, z, core), batch: 4 (over x).
Axes of the slice: x: 4, y: 4, z: 4, core: 2. Of those that a mesh axis runs over, the one named last changes fastest.
Arguments:
- queries: bfloat16 [4, 4096, 4096], P('batch', 'seq'), may hold values from -130 to 130
- keys: bfloat16 [4, 4096, 1024], P('batch', 'seq'), may hold values from -4 to 4
- values: bfloat16 [4, 4096, 1024], P('batch', 'seq'), may hold values from -4 to 4
- lengths: int32 [4], P('batch'), may hold values from 2048 to 4096
- block_pos: int32 [4, 32], P('batch'), may hold values from 0 to 31, each once within a row
- w_in: bfloat16 [6144, 1024], replicated, may hold values from -0.078125 to 0.078125
- b_in: float32 [1024], replicated, may hold values from -3 to 3
- output_weight: bfloat16 [1024, 8], replicated, may hold values from -0.1875 to 0.1875
- output_bias: float32 [8], replicated, may hold values from 1 to 2
Outputs:
- grad_w_in: float32 [6144, 1024], P(('seq', 'batch'))
- grad_b_in: float32 [1024], replicated
- output_weight_gradient: float32 [1024, 8], replicated
- output_bias_gradient: float32 [8], replicated
Inputs may be any that keep to these rules, and one draw needn't show every extreme that they name: Each row of block_pos names every block 0 to 31 once.
All inputs are finite; a program needn't handle non-finite values.
Results may differ from a plain program's by a relative error of at most 0.0017.
The roundings to bfloat16 on the way count: a program that leaves them out, or rounds other values in their place, can miss the bound.
Values may be sent and summed in bfloat16 or wider, within the bound.
No kernel may reach another device: no remote copies, remote signals or barrier semaphores. Data moves between devices by JAX's collectives and lax.ppermute only.
A program may use at most 128 MiB of HBM per device.

v0:
```python
import math
import jax
import jax.numpy as jnp
from jax import lax
from jax.sharding import PartitionSpec as P


def split_up(array, dim, size):
    before, after = (array.shape[:dim], array.shape[dim + 1 :])
    return jnp.moveaxis(array.reshape(*before, size, -1, *after), dim, 0)


def sent_and_summed(array, axis, dim):
    size = lax.axis_size(axis)
    tiles = lax.all_to_all(split_up(array, dim, size), axis, 0, 0, tiled=True)
    return jnp.sum(tiles, axis=0)


def in_one(arrays, axis):
    ends = [0]
    for a in arrays:
        ends.append(ends[-1] + a.size)
    so_far = lax.psum(jnp.concatenate([a.ravel() for a in arrays]), axis)
    return tuple((so_far[b:e].reshape(a.shape) for a, b, e in zip(arrays, ends, ends[1:])))


def on_device(queries, keys, values, lengths, block_pos, w_in, b_in, output_weight, output_bias):
    q_rows = queries[0]
    k_rows = keys[0]
    v_rows = values[0]
    rows = q_rows.shape[0]
    heads_kv = output_weight.shape[1]
    head_size = k_rows.shape[1] // heads_kv
    group_index = q_rows.shape[1] // k_rows.shape[1]
    scale = 1.0 / math.sqrt(head_size)
    every_key = lax.all_gather(k_rows, "seq", axis=0, tiled=True)
    total = every_key.shape[0]
    order = block_pos[0]
    offsets = jnp.arange(rows, dtype=jnp.int32)
    key_pos = (order[:, None] * rows + offsets[None, :]).reshape(-1)
    mine = lax.axis_index("seq")
    query_pos = lax.dynamic_index_in_dim(order, mine, 0, keepdims=False) * rows + offsets
    limit = lengths[0]
    allowed = (key_pos[None, :] <= query_pos[:, None]) & (key_pos < limit)[None, :]
    query_live = (query_pos < limit).astype(jnp.float32)

    def group_mass(index, sums):
        q_part = lax.dynamic_slice_in_dim(
            q_rows, index * group_index * head_size, group_index * head_size, 1
        )
        q_part = q_part.reshape(rows, group_index, head_size)
        k_part = lax.dynamic_slice_in_dim(every_key, index * head_size, head_size, 1)
        scores = (
            jnp.einsum("qhd,kd->hqk", q_part, k_part, preferred_element_type=jnp.float32) * scale
        )
        masked = jnp.where(allowed[None], scores, -1e30)
        top = jnp.max(masked, axis=2, keepdims=True)
        weights = jnp.where(allowed[None], jnp.exp(masked - top), 0.0)
        denom = jnp.sum(weights, axis=2, keepdims=True)
        share = weights / denom * query_live[None, :, None]
        column = jnp.sum(share, axis=(0, 1))
        return lax.dynamic_update_index_in_dim(sums, column, index, 0)

    partial_value = lax.fori_loop(
        0, heads_kv, group_mass, jnp.zeros((heads_kv, total), jnp.float32)
    )
    mass = sent_and_summed(partial_value, "seq", 1)
    labels = jnp.log1p(mass).T
    features = jnp.concatenate([q_rows, k_rows, v_rows], axis=1)
    pre = jnp.dot(features, w_in, preferred_element_type=jnp.float32) + b_in
    act = jax.nn.silu(pre).astype(jnp.bfloat16)
    pred = jnp.dot(act, output_weight, preferred_element_type=jnp.float32) + output_bias
    norm = 1.0 / math.sqrt(lax.axis_size("batch") * total)
    resid = ((pred - labels) * query_live[:, None] * norm).astype(jnp.bfloat16)
    back = lax.dot_general(
        resid, output_weight, (((1,), (1,)), ((), ())), preferred_element_type=jnp.float32
    )
    sig = jax.nn.sigmoid(pre)
    delta = (back * sig * (1.0 + pre * (1.0 - sig))).astype(jnp.bfloat16)
    out_term = lax.dot_general(
        act, resid, (((0,), (0,)), ((), ())), preferred_element_type=jnp.float32
    )
    grad_b_in, output_weight_gradient, output_bias_gradient = in_one(
        (
            jnp.sum(delta.astype(jnp.float32), axis=0),
            out_term,
            jnp.sum(resid.astype(jnp.float32), axis=0),
        ),
        ("seq", "batch"),
    )
    grad_w_in = lax.psum_scatter(
        lax.dot_general(
            features, delta, (((0,), (0,)), ((), ())), preferred_element_type=jnp.float32
        ),
        ("seq", "batch"),
        scatter_dimension=0,
        tiled=True,
    )
    return (grad_w_in, grad_b_in, output_weight_gradient, output_bias_gradient)


def solution(mesh):
    return jax.shard_map(
        on_device,
        mesh=mesh,
        in_specs=(
            P("batch", "seq", None),
            P("batch", "seq", None),
            P("batch", "seq", None),
            P("batch"),
            P("batch", None),
            P(),
            P(),
            P(),
            P(),
        ),
        out_specs=(P(("seq", "batch"), None), P(), P(), P()),
        check_vma=False,
    )
```

profile of v0, /device:TPU:0, one launch (start us, length us, event | category | flops | bytes accessed | tf_op | source)
XLA Modules:
  0.0 518.8 jit_solution(12301234503528148574)
XLA Ops:
  10.8 1.6 copy.14
  15.2 50.5 %all-gather.3.cloned.1.call-done = bf16[1,4096,1024]{2,1,0:T(8,128)(2,1)} async-done(((bf16[1,128,1024]{2,1,0:T(8,128)(2,1)}), bf16[1,4096,1024]{2,1,0:T(8,128)(2,1)}) %all-gather.3.cloned.1.call-update) | async-done | bytes 8388624 | tf_op jit(solution)/shard_map/all_gather | solution.py:36
  65.7 170.6 %while.16 = (s32[]{:T(128)}, f32[8,4096]{1,0:T(8,128)}, bf16[4096,1024]{1,0:T(8,128)(2,1)}, bf16[128,4096]{0,1:T(8,128)(2,1)S(1)}, s32[128]{0:T(128)S(1)}, /*ind...) while((s32[]{:T(128)}, f32[8,4096]{1,0:T(8,128)}, ...), condition=%wide.region_4.5_spmd.clone, body=%wide.region_0.4_spmd.clone.sunk | while | flops 1097869184 | bytes 22091528 | solution.py:64
  65.7 1.3 compare_convert_fusion.3
  67.0 1.4 compare_and_fusion.2
  68.4 8.6 %fusion.72 = f32[4,128,4096]{1,2,0:T(8,128)} fusion(pred[128,4096]{0,1:T(8,128)(4,1)S(1)} %compare_and_fusion.2, bf16[128,4,128]{0,2,1:T(8,128)(2,1)S(1)} %bitcast.69, bf16[4096,1024]{1,0:T(8,128)(2,1)} %get-tuple-element.300, s32[]{:T(128)S(6)} %select_n.79), kind=kOutput, calls=%fused_computation.2.clone.1 | convolution fusion | flops 545268736 | bytes 10616836 | tf_op jit(solution)/shard_map/while/body/eval_jaxpr/div | solution.py:60
  77.0 8.4 %multiply_reduce_fusion.2 = f32[4096]{0:T(1024)S(1)} fusion(f32[4,128,4096]{1,2,0:T(8,128)} %fusion.72, f32[128]{0:T(128)S(1)} %compare_convert_fusion.3, pred[128,4096]{0,1:T(8,128)(4,1)S(1)} %compare_and_fusion.2, bf16[128,4,128]{0,2,1:T(8,128)(2,1)S(1)} %bitcast.70, bf16[4096,1024]{1,0:T(8,128)(2,1)} %get-tuple-element.300, s32[]{:T(128)S(6)} %select_n.79), kind=kOutput, calls=%fused_computation.5.clone.1 | convolution fusion | flops 551551488 | bytes 10633732 | tf_op jit(solution)/shard_map/while/body/eval_jaxpr/sub | solution.py:58
  85.4 1.6 dynamic_update_slice.13
  87.0 1.3 compare_convert_fusion.3
  88.3 1.4 compare_and_fusion.2
  89.7 8.6 %fusion.72 = f32[4,128,4096]{1,2,0:T(8,128)} fusion(pred[128,4096]{0,1:T(8,128)(4,1)S(1)} %compare_and_fusion.2, bf16[128,4,128]{0,2,1:T(8,128)(2,1)S(1)} %bitcast.69, bf16[4096,1024]{1,0:T(8,128)(2,1)} %get-tuple-element.300, s32[]{:T(128)S(6)} %select_n.79), kind=kOutput, calls=%fused_computation.2.clone.1 | convolution fusion | flops 545268736 | bytes 10616836 | tf_op jit(solution)/shard_map/while/body/eval_jaxpr/div | solution.py:60
  98.3 8.4 %multiply_reduce_fusion.2 = f32[4096]{0:T(1024)S(1)} fusion(f32[4,128,4096]{1,2,0:T(8,128)} %fusion.72, f32[128]{0:T(128)S(1)} %compare_convert_fusion.3, pred[128,4096]{0,1:T(8,128)(4,1)S(1)} %compare_and_fusion.2, bf16[128,4,128]{0,2,1:T(8,128)(2,1)S(1)} %bitcast.70, bf16[4096,1024]{1,0:T(8,128)(2,1)} %get-tuple-element.300, s32[]{:T(128)S(6)} %select_n.79), kind=kOutput, calls=%fused_computation.5.clone.1 | convolution fusion | flops 551551488 | bytes 10633732 | tf_op jit(solution)/shard_map/while/body/eval_jaxpr/sub | solution.py:58
  106.7 1.6 dynamic_update_slice.13
  108.3 1.3 compare_convert_fusion.3
  109.6 1.4 compare_and_fusion.2
  111.0 8.6 %fusion.72 = f32[4,128,4096]{1,2,0:T(8,128)} fusion(pred[128,4096]{0,1:T(8,128)(4,1)S(1)} %compare_and_fusion.2, bf16[128,4,128]{0,2,1:T(8,128)(2,1)S(1)} %bitcast.69, bf16[4096,1024]{1,0:T(8,128)(2,1)} %get-tuple-element.300, s32[]{:T(128)S(6)} %select_n.79), kind=kOutput, calls=%fused_computation.2.clone.1 | convolution fusion | flops 545268736 | bytes 10616836 | tf_op jit(solution)/shard_map/while/body/eval_jaxpr/div | solution.py:60
  119.6 8.4 %multiply_reduce_fusion.2 = f32[4096]{0:T(1024)S(1)} fusion(f32[4,128,4096]{1,2,0:T(8,128)} %fusion.72, f32[128]{0:T(128)S(1)} %compare_convert_fusion.3, pred[128,4096]{0,1:T(8,128)(4,1)S(1)} %compare_and_fusion.2, bf16[128,4,128]{0,2,1:T(8,128)(2,1)S(1)} %bitcast.70, bf16[4096,1024]{1,0:T(8,128)(2,1)} %get-tuple-element.300, s32[]{:T(128)S(6)} %select_n.79), kind=kOutput, calls=%fused_computation.5.clone.1 | convolution fusion | flops 551551488 | bytes 10633732 | tf_op jit(solution)/shard_map/while/body/eval_jaxpr/sub | solution.py:58
  128.0 1.6 dynamic_update_slice.13
  129.6 1.3 compare_convert_fusion.3
  131.0 1.4 compare_and_fusion.2
  132.4 8.6 %fusion.72 = f32[4,128,4096]{1,2,0:T(8,128)} fusion(pred[128,4096]{0,1:T(8,128)(4,1)S(1)} %compare_and_fusion.2, bf16[128,4,128]{0,2,1:T(8,128)(2,1)S(1)} %bitcast.69, bf16[4096,1024]{1,0:T(8,128)(2,1)} %get-tuple-element.300, s32[]{:T(128)S(6)} %select_n.79), kind=kOutput, calls=%fused_computation.2.clone.1 | convolution fusion | flops 545268736 | bytes 10616836 | tf_op jit(solution)/shard_map/while/body/eval_jaxpr/div | solution.py:60
  141.0 8.4 %multiply_reduce_fusion.2 = f32[4096]{0:T(1024)S(1)} fusion(f32[4,128,4096]{1,2,0:T(8,128)} %fusion.72, f32[128]{0:T(128)S(1)} %compare_convert_fusion.3, pred[128,4096]{0,1:T(8,128)(4,1)S(1)} %compare_and_fusion.2, bf16[128,4,128]{0,2,1:T(8,128)(2,1)S(1)} %bitcast.70, bf16[4096,1024]{1,0:T(8,128)(2,1)} %get-tuple-element.300, s32[]{:T(128)S(6)} %select_n.79), kind=kOutput, calls=%fused_computation.5.clone.1 | convolution fusion | flops 551551488 | bytes 10633732 | tf_op jit(solution)/shard_map/while/body/eval_jaxpr/sub | solution.py:58
  149.3 1.6 dynamic_update_slice.13
  151.0 1.3 compare_convert_fusion.3
  152.3 1.4 compare_and_fusion.2
  153.7 8.6 %fusion.72 = f32[4,128,4096]{1,2,0:T(8,128)} fusion(pred[128,4096]{0,1:T(8,128)(4,1)S(1)} %compare_and_fusion.2, bf16[128,4,128]{0,2,1:T(8,128)(2,1)S(1)} %bitcast.69, bf16[4096,1024]{1,0:T(8,128)(2,1)} %get-tuple-element.300, s32[]{:T(128)S(6)} %select_n.79), kind=kOutput, calls=%fused_computation.2.clone.1 | convolution fusion | flops 545268736 | bytes 10616836 | tf_op jit(solution)/shard_map/while/body/eval_jaxpr/div | solution.py:60
  162.3 8.4 %multiply_reduce_fusion.2 = f32[4096]{0:T(1024)S(1)} fusion(f32[4,128,4096]{1,2,0:T(8,128)} %fusion.72, f32[128]{0:T(128)S(1)} %compare_convert_fusion.3, pred[128,4096]{0,1:T(8,128)(4,1)S(1)} %compare_and_fusion.2, bf16[128,4,128]{0,2,1:T(8,128)(2,1)S(1)} %bitcast.70, bf16[4096,1024]{1,0:T(8,128)(2,1)} %get-tuple-element.300, s32[]{:T(128)S(6)} %select_n.79), kind=kOutput, calls=%fused_computation.5.clone.1 | convolution fusion | flops 551551488 | bytes 10633732 | tf_op jit(solution)/shard_map/while/body/eval_jaxpr/sub | solution.py:58
  170.7 1.6 dynamic_update_slice.13
  172.3 1.3 compare_convert_fusion.3
  173.6 1.4 compare_and_fusion.2
  175.0 8.6 %fusion.72 = f32[4,128,4096]{1,2,0:T(8,128)} fusion(pred[128,4096]{0,1:T(8,128)(4,1)S(1)} %compare_and_fusion.2, bf16[128,4,128]{0,2,1:T(8,128)(2,1)S(1)} %bitcast.69, bf16[4096,1024]{1,0:T(8,128)(2,1)} %get-tuple-element.300, s32[]{:T(128)S(6)} %select_n.79), kind=kOutput, calls=%fused_computation.2.clone.1 | convolution fusion | flops 545268736 | bytes 10616836 | tf_op jit(solution)/shard_map/while/body/eval_jaxpr/div | solution.py:60
  183.6 8.4 %multiply_reduce_fusion.2 = f32[4096]{0:T(1024)S(1)} fusion(f32[4,128,4096]{1,2,0:T(8,128)} %fusion.72, f32[128]{0:T(128)S(1)} %compare_convert_fusion.3, pred[128,4096]{0,1:T(8,128)(4,1)S(1)} %compare_and_fusion.2, bf16[128,4,128]{0,2,1:T(8,128)(2,1)S(1)} %bitcast.70, bf16[4096,1024]{1,0:T(8,128)(2,1)} %get-tuple-element.300, s32[]{:T(128)S(6)} %select_n.79), kind=kOutput, calls=%fused_computation.5.clone.1 | convolution fusion | flops 551551488 | bytes 10633732 | tf_op jit(solution)/shard_map/while/body/eval_jaxpr/sub | solution.py:58
  192.0 1.6 dynamic_update_slice.13
  193.6 1.3 compare_convert_fusion.3
  194.9 1.4 compare_and_fusion.2
  196.3 8.6 %fusion.72 = f32[4,128,4096]{1,2,0:T(8,128)} fusion(pred[128,4096]{0,1:T(8,128)(4,1)S(1)} %compare_and_fusion.2, bf16[128,4,128]{0,2,1:T(8,128)(2,1)S(1)} %bitcast.69, bf16[4096,1024]{1,0:T(8,128)(2,1)} %get-tuple-element.300, s32[]{:T(128)S(6)} %select_n.79), kind=kOutput, calls=%fused_computation.2.clone.1 | convolution fusion | flops 545268736 | bytes 10616836 | tf_op jit(solution)/shard_map/while/body/eval_jaxpr/div | solution.py:60
  204.9 8.4 %multiply_reduce_fusion.2 = f32[4096]{0:T(1024)S(1)} fusion(f32[4,128,4096]{1,2,0:T(8,128)} %fusion.72, f32[128]{0:T(128)S(1)} %compare_convert_fusion.3, pred[128,4096]{0,1:T(8,128)(4,1)S(1)} %compare_and_fusion.2, bf16[128,4,128]{0,2,1:T(8,128)(2,1)S(1)} %bitcast.70, bf16[4096,1024]{1,0:T(8,128)(2,1)} %get-tuple-element.300, s32[]{:T(128)S(6)} %select_n.79), kind=kOutput, calls=%fused_computation.5.clone.1 | convolution fusion | flops 551551488 | bytes 10633732 | tf_op jit(solution)/shard_map/while/body/eval_jaxpr/sub | solution.py:58
  213.3 1.6 dynamic_update_slice.13
  214.9 1.3 compare_convert_fusion.3
  216.2 1.4 compare_and_fusion.2
  217.6 8.6 %fusion.72 = f32[4,128,4096]{1,2,0:T(8,128)} fusion(pred[128,4096]{0,1:T(8,128)(4,1)S(1)} %compare_and_fusion.2, bf16[128,4,128]{0,2,1:T(8,128)(2,1)S(1)} %bitcast.69, bf16[4096,1024]{1,0:T(8,128)(2,1)} %get-tuple-element.300, s32[]{:T(128)S(6)} %select_n.79), kind=kOutput, calls=%fused_computation.2.clone.1 | convolution fusion | flops 545268736 | bytes 10616836 | tf_op jit(solution)/shard_map/while/body/eval_jaxpr/div | solution.py:60
  226.2 8.4 %multiply_reduce_fusion.2 = f32[4096]{0:T(1024)S(1)} fusion(f32[4,128,4096]{1,2,0:T(8,128)} %fusion.72, f32[128]{0:T(128)S(1)} %compare_convert_fusion.3, pred[128,4096]{0,1:T(8,128)(4,1)S(1)} %compare_and_fusion.2, bf16[128,4,128]{0,2,1:T(8,128)(2,1)S(1)} %bitcast.70, bf16[4096,1024]{1,0:T(8,128)(2,1)} %get-tuple-element.300, s32[]{:T(128)S(6)} %select_n.79), kind=kOutput, calls=%fused_computation.5.clone.1 | convolution fusion | flops 551551488 | bytes 10633732 | tf_op jit(solution)/shard_map/while/body/eval_jaxpr/sub | solution.py:58
  234.6 1.6 dynamic_update_slice.13
  236.2 5.5 %all-to-all-start = ((f32[32,8,128]{2,1,0:T(8,128)}), f32[32,8,128]{2,1,0:T(8,128)S(1)}, u32[]{:S(2)}, u32[]{:S(2)}) async-start(f32[32,8,128]{2,1,0:T(8,128)} %bitcast.9), calls=%async_computation | async-start | bytes 262144 | tf_op jit(solution)/shard_map/all_to_all | solution.py:15
  242.0 6.5 %multiply_convert_fusion = (bf16[128,1024]{1,0:T(8,128)(2,1)S(1)}, f32[128,1024]{1,0:T(8,128)S(1)}) fusion(f32[1024]{0:T(1024)S(1)} %copy-done.1, bf16[6144,1024]{1,0:T(8,128)(2,1)} %param.16, bf16[128,1024]{0,1:T(8,128)(2,1)S(1)} %bitcast.73, bf16[128,1024]{0,1:T(8,128)(2,1)S(1)} %bitcast.71, bf16[128,4096]{0,1:T(8,128)(2,1)S(1)} %get-tuple-element.317), kind=kOutput, calls=%fused_computation.42 | convolution fusion | flops 1616117760 | bytes 14946304 | tf_op jit(solution)/shard_map/dot_general | solution.py:70
  250.3 13.2 %fusion.46 = f32[6144,1024]{1,0:T(8,128)} fusion(bf16[128,1024]{1,0:T(8,128)(2,1)S(1)} %get-tuple-element.212, bf16[128,1024]{0,1:T(8,128)(2,1)S(1)} %bitcast.74, bf16[128,1024]{0,1:T(8,128)(2,1)S(1)} %bitcast.72, bf16[128,4096]{0,1:T(8,128)(2,1)S(1)} %get-tuple-element.317), kind=kOutput, calls=%fused_computation.40 | convolution fusion | flops 1615331328 | bytes 27000832 | tf_op jit(solution)/shard_map/dot_general | solution.py:92
  264.1 67.0 %psum.7 = f32[9224]{0:T(1024)S(1)} all-reduce(f32[9224]{0:T(1024)S(1)} %pad_maximum_fusion.3), channel_id=1, replica_groups=mesh['seq'=32,'batch'=4] {'seq','batch'}, use_global_device_ids=true, to_apply=%region_9.10 | all-reduce | flops 9224 | bytes 73792 | tf_op jit(solution)/shard_map/psum | solution.py:23
  333.2 178.8 %reduce-scatter.2.cloned.1.call-done = f32[48,1024]{1,0:T(8,128)} async-done(((f32[6144,1024]{1,0:T(8,128)}), f32[48,1024]{1,0:T(8,128)}) %reduce-scatter.2.cloned.1.call-update) | async-done | bytes 196624 | tf_op jit(solution)/shard_map/reduce_scatter | solution.py:91
  (39 shorter events, 10.5 us)
Async XLA Ops:
  7.2 242.5 %copy-start = (bf16[1024,8]{0,1:T(8,128)(2,1)S(1)}, bf16[1024,8]{0,1:T(8,128)(2,1)}, u32[]{:S(2)}) copy-start(bf16[1024,8]{0,1:T(8,128)(2,1)} %param.18) | copy-start | bytes 49156
  7.2 58.5 %all-gather.3.cloned.1.call-start = ((), (), s32[]{:S(2)}) async-start(), calls=%async_computation.3 | async-start | bytes 8650752 | tf_op jit(solution)/shard_map/all_gather | solution.py:36
  65.7 176.3 %copy-start.1 = (f32[1024]{0:T(1024)S(1)}, f32[1024]{0:T(1024)}, u32[]{:S(2)}) copy-start(f32[1024]{0:T(1024)} %param.17) | copy-start | bytes 12292
  236.2 13.3 %all-to-all-start = ((f32[32,8,128]{2,1,0:T(8,128)}), f32[32,8,128]{2,1,0:T(8,128)S(1)}, u32[]{:S(2)}, u32[]{:S(2)}) async-start(f32[32,8,128]{2,1,0:T(8,128)} %bitcast.9), calls=%async_computation | async-start | bytes 262144 | tf_op jit(solution)/shard_map/all_to_all | solution.py:15
  241.7 270.2 %reduce-scatter.2.cloned.1.call-start = ((), (), s32[]{:S(2)}) async-start(), calls=%async_computation.2 | async-start | bytes 25362432 | tf_op jit(solution)/shard_map/reduce_scatter | solution.py:91
  242.0 7.6 %copy-start.2 = (f32[8]{0:T(128)S(1)}, f32[8]{0:T(128)}, u32[]{:S(2)}) copy-start(f32[8]{0:T(128)} %param.19) | copy-start | bytes 100
Sparse Core Ops, SparseCore 0:
  10.3 55.3 all-gather.2
  263.7 248.2 reduce-scatter.1
where the time goes:
time: 520 us; the launch traced here: 519 us
  waiting for transfers between devices  230 us (44%)
  matrix products  156 us (30%)
  blocking collectives  67 us (13%)
  other arithmetic  24.9 us (5%)
  local copies, waits for them, and re-layouts  19.4 us (4%)
  between operations  14.8 us (3%)
  starting transfers between devices  5.76 us (1%)
    reduce_scatter x1, waiting for transfers between devices, on_device(): lax.psum_scatter(lax.dot_general(features, delta, (((0,), (0,)), ((), ())...  179 us
    div x8, matrix products, group_mass(): share = weights / denom * query_live[None, :, None]  68.8 us
    sub x8, matrix products, group_mass(): weights = jnp.where(allowed[None], jnp.exp(masked - top), 0.0)  67 us
    psum x1, blocking collectives, in_one(): so_far = lax.psum(jnp.concatenate([a.ravel() for a in arrays]), axis)  67 us
    all_gather x1, waiting for transfers between devices, on_device(): every_key = lax.all_gather(k_rows, 'seq', axis=0, tiled=True)  50.5 us
    dot_general x1, matrix products, on_device(): lax.dot_general(features, delta, (((0,), (0,)), ((), ())), preferred_elem...  13.2 us
    dynamic_update_slice x8, local copies, waits for them, and re-layouts, group_mass(): return lax.dynamic_update_index_in_dim(sums, column, index, 0)  12.9 us
    and x8, other arithmetic, on_device(): (key_pos[None, :] <= query_pos[:, None]) & (key_pos < limit)[None, :]  11.1 us
  transfers between devices with their start and end apart: 3, of which 3 were waited for; matrix products, arithmetic and copies ran while one was open for 3% of the time, Pallas kernels for 0%

commit v1 on v0

--- a/solution.py
+++ b/solution.py
@@ -20,7 +20,7 @@
     ends = [0]
     for a in arrays:
         ends.append(ends[-1] + a.size)
-    so_far = lax.psum(jnp.concatenate([a.ravel() for a in arrays]), axis)
+    so_far = jnp.sum(lax.all_gather(jnp.concatenate([a.ravel() for a in arrays]), axis), axis=0)
     return tuple((so_far[b:e].reshape(a.shape) for a, b, e in zip(arrays, ends, ends[1:])))
 
 

time: 520 us -> 671 us (1.29)
  waiting for transfers between devices: 230 us -> 434 us
  blocking collectives: 67 us -> 0 us
  local copies, waits for them, and re-layouts: 19.4 us -> 29.1 us
    unnamed x2 -> x4, waiting for transfers between devices: 0.7 us -> 144 us
    psum x1 -> x0, blocking collectives: 67 us -> none  [in_one(): so_far = lax.psum(jnp.concatenate([a.ravel() for a in arrays]), axis)]
    reduce_scatter x1, waiting for transfers between devices: 179 us -> 240 us  [on_device(): lax.psum_scatter(lax.dot_general(features, delta, (((0,), (0,)), ((), ())...]
    all_gather x0 -> x1, local copies, waits for them, and re-layouts: none -> 7.43 us  [in_one(): lax.all_gather(jnp.concatenate([a.ravel() for a in arrays]), axis)]
  transfers between devices with their start and end apart: 3 -> 4, of which waited for: 3 -> 4; matrix products, arithmetic and copies ran while one was open for 3% -> 6% of each run, Pallas kernels for 0% -> 0%
where the time goes in v1:
time: 671 us; the launch traced here: 670 us
  waiting for transfers between devices  434 us (65%)
  matrix products  157 us (23%)
  local copies, waits for them, and re-layouts  29.1 us (4%)
  other arithmetic  29 us (4%)
  between operations  14.5 us (2%)
    reduce_scatter x1, waiting for transfers between devices, on_device(): lax.psum_scatter(lax.dot_general(features, delta, (((0,), (0,)), ((), ())...  240 us
    unnamed x4, waiting for transfers between devices  144 us
    div x8, matrix products, group_mass(): share = weights / denom * query_live[None, :, None]  68.9 us
    sub x8, matrix products, group_mass(): weights = jnp.where(allowed[None], jnp.exp(masked - top), 0.0)  67.3 us
    all_gather x1, waiting for transfers between devices, on_device(): every_key = lax.all_gather(k_rows, 'seq', axis=0, tiled=True)  50.5 us
  transfers between devices with their start and end apart: 4, of which 4 were waited for; matrix products, arithmetic and copies ran while one was open for 6% of the time, Pallas kernels for 0%

profile of v1, /device:TPU:0, one launch (start us, length us, event | category | flops | bytes accessed | tf_op | source)
XLA Modules:
  0.0 669.9 jit_solution(6783217785189078675)
XLA Ops:
  10.8 1.6 copy.14
  15.2 50.5 %all-gather.4.cloned.1.call-done = bf16[1,4096,1024]{2,1,0:T(8,128)(2,1)} async-done(((bf16[1,128,1024]{2,1,0:T(8,128)(2,1)}), bf16[1,4096,1024]{2,1,0:T(8,128)(2,1)}) %all-gather.4.cloned.1.call-update) | async-done | bytes 8388624 | tf_op jit(solution)/shard_map/all_gather | solution.py:36
  65.7 171.1 %while.16 = (s32[]{:T(128)}, f32[8,4096]{1,0:T(8,128)}, bf16[4096,1024]{1,0:T(8,128)(2,1)}, bf16[128,4096]{0,1:T(8,128)(2,1)S(1)}, s32[128]{0:T(128)S(1)}, /*ind...) while((s32[]{:T(128)}, f32[8,4096]{1,0:T(8,128)}, ...), condition=%wide.region_4.5_spmd.clone, body=%wide.region_0.4_spmd.clone.sunk | while | flops 1097869184 | bytes 22091528 | solution.py:64
  65.7 1.3 compare_convert_fusion.3
  67.0 1.4 compare_and_fusion.2
  68.4 8.6 %fusion.72 = f32[4,128,4096]{1,2,0:T(8,128)} fusion(pred[128,4096]{0,1:T(8,128)(4,1)S(1)} %compare_and_fusion.2, bf16[128,4,128]{0,2,1:T(8,128)(2,1)S(1)} %bitcast.69, bf16[4096,1024]{1,0:T(8,128)(2,1)} %get-tuple-element.300, s32[]{:T(128)S(6)} %select_n.79), kind=kOutput, calls=%fused_computation.2.clone.1 | convolution fusion | flops 545268736 | bytes 10616836 | tf_op jit(solution)/shard_map/while/body/eval_jaxpr/div | solution.py:60
  77.0 8.4 %multiply_reduce_fusion.2 = f32[4096]{0:T(1024)S(1)} fusion(f32[4,128,4096]{1,2,0:T(8,128)} %fusion.72, f32[128]{0:T(128)S(1)} %compare_convert_fusion.3, pred[128,4096]{0,1:T(8,128)(4,1)S(1)} %compare_and_fusion.2, bf16[128,4,128]{0,2,1:T(8,128)(2,1)S(1)} %bitcast.70, bf16[4096,1024]{1,0:T(8,128)(2,1)} %get-tuple-element.300, s32[]{:T(128)S(6)} %select_n.79), kind=kOutput, calls=%fused_computation.5.clone.1 | convolution fusion | flops 551551488 | bytes 10633732 | tf_op jit(solution)/shard_map/while/body/eval_jaxpr/sub | solution.py:58
  85.4 1.6 dynamic_update_slice.13
  87.1 1.3 compare_convert_fusion.3
  88.4 1.4 compare_and_fusion.2
  89.8 8.6 %fusion.72 = f32[4,128,4096]{1,2,0:T(8,128)} fusion(pred[128,4096]{0,1:T(8,128)(4,1)S(1)} %compare_and_fusion.2, bf16[128,4,128]{0,2,1:T(8,128)(2,1)S(1)} %bitcast.69, bf16[4096,1024]{1,0:T(8,128)(2,1)} %get-tuple-element.300, s32[]{:T(128)S(6)} %select_n.79), kind=kOutput, calls=%fused_computation.2.clone.1 | convolution fusion | flops 545268736 | bytes 10616836 | tf_op jit(solution)/shard_map/while/body/eval_jaxpr/div | solution.py:60
  98.4 8.4 %multiply_reduce_fusion.2 = f32[4096]{0:T(1024)S(1)} fusion(f32[4,128,4096]{1,2,0:T(8,128)} %fusion.72, f32[128]{0:T(128)S(1)} %compare_convert_fusion.3, pred[128,4096]{0,1:T(8,128)(4,1)S(1)} %compare_and_fusion.2, bf16[128,4,128]{0,2,1:T(8,128)(2,1)S(1)} %bitcast.70, bf16[4096,1024]{1,0:T(8,128)(2,1)} %get-tuple-element.300, s32[]{:T(128)S(6)} %select_n.79), kind=kOutput, calls=%fused_computation.5.clone.1 | convolution fusion | flops 551551488 | bytes 10633732 | tf_op jit(solution)/shard_map/while/body/eval_jaxpr/sub | solution.py:58
  106.8 1.6 dynamic_update_slice.13
  108.4 1.3 compare_convert_fusion.3
  109.8 1.4 compare_and_fusion.2
  111.2 8.6 %fusion.72 = f32[4,128,4096]{1,2,0:T(8,128)} fusion(pred[128,4096]{0,1:T(8,128)(4,1)S(1)} %compare_and_fusion.2, bf16[128,4,128]{0,2,1:T(8,128)(2,1)S(1)} %bitcast.69, bf16[4096,1024]{1,0:T(8,128)(2,1)} %get-tuple-element.300, s32[]{:T(128)S(6)} %select_n.79), kind=kOutput, calls=%fused_computation.2.clone.1 | convolution fusion | flops 545268736 | bytes 10616836 | tf_op jit(solution)/shard_map/while/body/eval_jaxpr/div | solution.py:60
  119.8 8.4 %multiply_reduce_fusion.2 = f32[4096]{0:T(1024)S(1)} fusion(f32[4,128,4096]{1,2,0:T(8,128)} %fusion.72, f32[128]{0:T(128)S(1)} %compare_convert_fusion.3, pred[128,4096]{0,1:T(8,128)(4,1)S(1)} %compare_and_fusion.2, bf16[128,4,128]{0,2,1:T(8,128)(2,1)S(1)} %bitcast.70, bf16[4096,1024]{1,0:T(8,128)(2,1)} %get-tuple-element.300, s32[]{:T(128)S(6)} %select_n.79), kind=kOutput, calls=%fused_computation.5.clone.1 | convolution fusion | flops 551551488 | bytes 10633732 | tf_op jit(solution)/shard_map/while/body/eval_jaxpr/sub | solution.py:58
  128.2 1.6 dynamic_update_slice.13
  131.1 1.4 compare_and_fusion.2
  132.5 8.6 %fusion.72 = f32[4,128,4096]{1,2,0:T(8,128)} fusion(pred[128,4096]{0,1:T(8,128)(4,1)S(1)} %compare_and_fusion.2, bf16[128,4,128]{0,2,1:T(8,128)(2,1)S(1)} %bitcast.69, bf16[4096,1024]{1,0:T(8,128)(2,1)} %get-tuple-element.300, s32[]{:T(128)S(6)} %select_n.79), kind=kOutput, calls=%fused_computation.2.clone.1 | convolution fusion | flops 545268736 | bytes 10616836 | tf_op jit(solution)/shard_map/while/body/eval_jaxpr/div | solution.py:60
  141.2 8.4 %multiply_reduce_fusion.2 = f32[4096]{0:T(1024)S(1)} fusion(f32[4,128,4096]{1,2,0:T(8,128)} %fusion.72, f32[128]{0:T(128)S(1)} %compare_convert_fusion.3, pred[128,4096]{0,1:T(8,128)(4,1)S(1)} %compare_and_fusion.2, bf16[128,4,128]{0,2,1:T(8,128)(2,1)S(1)} %bitcast.70, bf16[4096,1024]{1,0:T(8,128)(2,1)} %get-tuple-element.300, s32[]{:T(128)S(6)} %select_n.79), kind=kOutput, calls=%fused_computation.5.clone.1 | convolution fusion | flops 551551488 | bytes 10633732 | tf_op jit(solution)/shard_map/while/body/eval_jaxpr/sub | solution.py:58
  149.6 1.6 dynamic_update_slice.13
  151.2 1.3 compare_convert_fusion.3
  152.5 1.4 compare_and_fusion.2
  153.9 8.6 %fusion.72 = f32[4,128,4096]{1,2,0:T(8,128)} fusion(pred[128,4096]{0,1:T(8,128)(4,1)S(1)} %compare_and_fusion.2, bf16[128,4,128]{0,2,1:T(8,128)(2,1)S(1)} %bitcast.69, bf16[4096,1024]{1,0:T(8,128)(2,1)} %get-tuple-element.300, s32[]{:T(128)S(6)} %select_n.79), kind=kOutput, calls=%fused_computation.2.clone.1 | convolution fusion | flops 545268736 | bytes 10616836 | tf_op jit(solution)/shard_map/while/body/eval_jaxpr/div | solution.py:60
  162.5 8.4 %multiply_reduce_fusion.2 = f32[4096]{0:T(1024)S(1)} fusion(f32[4,128,4096]{1,2,0:T(8,128)} %fusion.72, f32[128]{0:T(128)S(1)} %compare_convert_fusion.3, pred[128,4096]{0,1:T(8,128)(4,1)S(1)} %compare_and_fusion.2, bf16[128,4,128]{0,2,1:T(8,128)(2,1)S(1)} %bitcast.70, bf16[4096,1024]{1,0:T(8,128)(2,1)} %get-tuple-element.300, s32[]{:T(128)S(6)} %select_n.79), kind=kOutput, calls=%fused_computation.5.clone.1 | convolution fusion | flops 551551488 | bytes 10633732 | tf_op jit(solution)/shard_map/while/body/eval_jaxpr/sub | solution.py:58
  171.0 1.6 dynamic_update_slice.13
  173.9 1.4 compare_and_fusion.2
  175.3 8.6 %fusion.72 = f32[4,128,4096]{1,2,0:T(8,128)} fusion(pred[128,4096]{0,1:T(8,128)(4,1)S(1)} %compare_and_fusion.2, bf16[128,4,128]{0,2,1:T(8,128)(2,1)S(1)} %bitcast.69, bf16[4096,1024]{1,0:T(8,128)(2,1)} %get-tuple-element.300, s32[]{:T(128)S(6)} %select_n.79), kind=kOutput, calls=%fused_computation.2.clone.1 | convolution fusion | flops 545268736 | bytes 10616836 | tf_op jit(solution)/shard_map/while/body/eval_jaxpr/div | solution.py:60
  183.9 8.4 %multiply_reduce_fusion.2 = f32[4096]{0:T(1024)S(1)} fusion(f32[4,128,4096]{1,2,0:T(8,128)} %fusion.72, f32[128]{0:T(128)S(1)} %compare_convert_fusion.3, pred[128,4096]{0,1:T(8,128)(4,1)S(1)} %compare_and_fusion.2, bf16[128,4,128]{0,2,1:T(8,128)(2,1)S(1)} %bitcast.70, bf16[4096,1024]{1,0:T(8,128)(2,1)} %get-tuple-element.300, s32[]{:T(128)S(6)} %select_n.79), kind=kOutput, calls=%fused_computation.5.clone.1 | convolution fusion | flops 551551488 | bytes 10633732 | tf_op jit(solution)/shard_map/while/body/eval_jaxpr/sub | solution.py:58
  192.3 1.6 dynamic_update_slice.13
  195.3 1.4 compare_and_fusion.2
  196.7 8.6 %fusion.72 = f32[4,128,4096]{1,2,0:T(8,128)} fusion(pred[128,4096]{0,1:T(8,128)(4,1)S(1)} %compare_and_fusion.2, bf16[128,4,128]{0,2,1:T(8,128)(2,1)S(1)} %bitcast.69, bf16[4096,1024]{1,0:T(8,128)(2,1)} %get-tuple-element.300, s32[]{:T(128)S(6)} %select_n.79), kind=kOutput, calls=%fused_computation.2.clone.1 | convolution fusion | flops 545268736 | bytes 10616836 | tf_op jit(solution)/shard_map/while/body/eval_jaxpr/div | solution.py:60
  205.3 8.4 %multiply_reduce_fusion.2 = f32[4096]{0:T(1024)S(1)} fusion(f32[4,128,4096]{1,2,0:T(8,128)} %fusion.72, f32[128]{0:T(128)S(1)} %compare_convert_fusion.3, pred[128,4096]{0,1:T(8,128)(4,1)S(1)} %compare_and_fusion.2, bf16[128,4,128]{0,2,1:T(8,128)(2,1)S(1)} %bitcast.70, bf16[4096,1024]{1,0:T(8,128)(2,1)} %get-tuple-element.300, s32[]{:T(128)S(6)} %select_n.79), kind=kOutput, calls=%fused_computation.5.clone.1 | convolution fusion | flops 551551488 | bytes 10633732 | tf_op jit(solution)/shard_map/while/body/eval_jaxpr/sub | solution.py:58
  213.7 1.6 dynamic_update_slice.13
  216.7 1.4 compare_and_fusion.2
  218.1 8.6 %fusion.72 = f32[4,128,4096]{1,2,0:T(8,128)} fusion(pred[128,4096]{0,1:T(8,128)(4,1)S(1)} %compare_and_fusion.2, bf16[128,4,128]{0,2,1:T(8,128)(2,1)S(1)} %bitcast.69, bf16[4096,1024]{1,0:T(8,128)(2,1)} %get-tuple-element.300, s32[]{:T(128)S(6)} %select_n.79), kind=kOutput, calls=%fused_computation.2.clone.1 | convolution fusion | flops 545268736 | bytes 10616836 | tf_op jit(solution)/shard_map/while/body/eval_jaxpr/div | solution.py:60
  226.7 8.4 %multiply_reduce_fusion.2 = f32[4096]{0:T(1024)S(1)} fusion(f32[4,128,4096]{1,2,0:T(8,128)} %fusion.72, f32[128]{0:T(128)S(1)} %compare_convert_fusion.3, pred[128,4096]{0,1:T(8,128)(4,1)S(1)} %compare_and_fusion.2, bf16[128,4,128]{0,2,1:T(8,128)(2,1)S(1)} %bitcast.70, bf16[4096,1024]{1,0:T(8,128)(2,1)} %get-tuple-element.300, s32[]{:T(128)S(6)} %select_n.79), kind=kOutput, calls=%fused_computation.5.clone.1 | convolution fusion | flops 551551488 | bytes 10633732 | tf_op jit(solution)/shard_map/while/body/eval_jaxpr/sub | solution.py:58
  235.1 1.6 dynamic_update_slice.13
  236.7 5.5 all-to-all-start
  242.5 6.5 multiply_convert_fusion
  251.3 2.3 broadcast.49
  253.6 1.5 maximum_dynamic-update-slice_fusion
  255.2 13.2 %fusion.46 = f32[6144,1024]{1,0:T(8,128)} fusion(bf16[128,1024]{1,0:T(8,128)(2,1)S(1)} %get-tuple-element.212, bf16[128,1024]{0,1:T(8,128)(2,1)S(1)} %bitcast.74, bf16[128,1024]{0,1:T(8,128)(2,1)S(1)} %bitcast.72, bf16[128,4096]{0,1:T(8,128)(2,1)S(1)} %get-tuple-element.318), kind=kOutput, calls=%fused_computation.40 | convolution fusion | flops 1615331328 | bytes 27000832 | tf_op jit(solution)/shard_map/dot_general | solution.py:92
  268.4 142.8 %all-reduce.3.cloned.1.call-done = f32[1180672]{0:T(1024)} async-done(((f32[1180672]{0:T(1024)}), f32[1180672]{0:T(1024)}) %all-reduce.3.cloned.1.call-update) | async-done | bytes 4722704
  411.2 7.4 %reshape.90 = f32[128,9224]{1,0:T(8,128)} reshape(f32[1180672]{0:T(1024)} %all-reduce.3.cloned.1.call-done) | data formatting | bytes 9445376 | tf_op jit(solution)/shard_map/all_gather | solution.py:23
  418.7 2.6 reduce_sum.71
  423.5 239.9 %reduce-scatter.2.cloned.1.call-done = f32[48,1024]{1,0:T(8,128)} async-done(((f32[6144,1024]{1,0:T(8,128)}), f32[48,1024]{1,0:T(8,128)}) %reduce-scatter.2.cloned.1.call-update) | async-done | bytes 196624 | tf_op jit(solution)/shard_map/reduce_scatter | solution.py:91
  (44 shorter events, 15.8 us)
Async XLA Ops:
  7.2 242.9 %copy-start = (bf16[1024,8]{0,1:T(8,128)(2,1)S(1)}, bf16[1024,8]{0,1:T(8,128)(2,1)}, u32[]{:S(2)}) copy-start(bf16[1024,8]{0,1:T(8,128)(2,1)} %param.18) | copy-start | bytes 49156
  7.2 58.5 %all-gather.4.cloned.1.call-start = ((), (), s32[]{:S(2)}) async-start(), calls=%async_computation.3 | async-start | bytes 8650752 | tf_op jit(solution)/shard_map/all_gather | solution.py:36
  65.7 176.8 %copy-start.1 = (f32[1024]{0:T(1024)S(1)}, f32[1024]{0:T(1024)}, u32[]{:S(2)}) copy-start(f32[1024]{0:T(1024)} %param.17) | copy-start | bytes 12292
  236.7 13.3 %all-to-all-start = ((f32[32,8,128]{2,1,0:T(8,128)}), f32[32,8,128]{2,1,0:T(8,128)S(1)}, u32[]{:S(2)}, u32[]{:S(2)}) async-start(f32[32,8,128]{2,1,0:T(8,128)} %bitcast.9), calls=%async_computation | async-start | bytes 262144 | tf_op jit(solution)/shard_map/all_to_all | solution.py:15
  242.2 169.0 %all-reduce.3.cloned.1.call-start = ((), (), s32[]{:S(2)}) async-start(), calls=%async_computation.4 | async-start | bytes 9445376
  242.5 7.6 %copy-start.2 = (f32[8]{0:T(128)S(1)}, f32[8]{0:T(128)}, u32[]{:S(2)}) copy-start(f32[8]{0:T(128)} %param.19) | copy-start | bytes 100
  255.1 408.3 %reduce-scatter.2.cloned.1.call-start = ((), (), s32[]{:S(2)}) async-start(), calls=%async_computation.2 | async-start | bytes 25362432 | tf_op jit(solution)/shard_map/reduce_scatter | solution.py:91
Sparse Core Ops, SparseCore 0:
  10.3 55.3 all-gather.3
  255.2 155.9 all-reduce.2
  417.1 246.2 reduce-scatter.1
